TPU v7x, 256 devices: a whole 4x4x8 slice. The times are simulated.
256 devices in a mesh: wide: 32 (over z, x), narrow: 8 (over y, core).
Axes of the slice: x: 4, y: 4, z: 8, core: 2. Of those that a mesh axis runs over, the one named last changes fastest.
Arguments:
- payload: bfloat16 [1048576, 128], P(('wide', 'narrow')), may hold values from -6 to 6
- first_key: int32 [1048576], P(('wide', 'narrow')), may hold values from 0 to 1073741823
- second_key: int32 [1048576], P(('wide', 'narrow')), may hold values from 0 to 1073741823
- live: int32 [1048576], P(('wide', 'narrow')), may hold values from 0 to 1
- first_bucket: int32 [1048576], P(('wide', 'narrow')), may hold values from 0 to 31, as said below
- second_bucket: int32 [1048576], P(('wide', 'narrow')), may hold values from 0 to 7
Outputs:
- group_mean: bfloat16 [1048576, 128], P(('wide', 'narrow'))
- duplicate_count: int32 [], replicated
Inputs may be any that keep to these rules, and one draw needn't show every extreme that they name: Each device's rows name each pair (first_bucket, second_bucket) exactly 16 times; in every draw there is one bucket pair all of whose rows survive; other rows survive or not as `live` says.
All inputs are finite; a program needn't handle non-finite values.
Results may differ from a plain program's by a relative error of at most 0.001.
Values may be sent and summed in bfloat16 or wider, within the bound.
A program may use at most 64 MiB of HBM per device.

v0:
```python
import jax
import jax.numpy as jnp
from jax import lax
from jax.sharding import Mesh
from jax.sharding import PartitionSpec as P

WIDE = ("wide_0", "wide_1")
NARROW = ("narrow_0", "narrow_1")
WIDE_NARROW = ("wide_0", "wide_1", "narrow_0", "narrow_1")


def in_blocks(array, dim, length):
    lengths = array.shape
    pieces = array.reshape(*lengths[:dim], length, lengths[dim] // length, *lengths[dim + 1 :])
    return jnp.moveaxis(pieces, dim, 0)


def joined_along(pieces, dim):
    lengths = list(pieces.shape[1:])
    lengths[dim] *= pieces.shape[0]
    return jnp.moveaxis(pieces, 0, dim).reshape(lengths)


def joined_exchange(array, axis, axes, splits, concats):
    sizes = [lax.axis_size(a) for a in axes]
    pieces = in_blocks(array, splits[0], sizes[0])
    pieces = jnp.moveaxis(in_blocks(pieces, splits[1] + 1, sizes[1]), 0, 1)
    inside = pieces.shape[2:]
    pieces = pieces.reshape(-1, *inside)
    pieces = lax.all_to_all(pieces, axis, split_axis=0, concat_axis=0, tiled=True)
    pieces = joined_along(pieces.reshape(*sizes, *inside), concats[0] + 1)
    return joined_along(pieces, concats[1])


def by_axis(array, axes):
    for axis in axes:
        array = lax.psum(array, axis)
    return array


def pair_mask(row_one, row_two, row_live, col_one, col_two, col_live):
    return (
        (row_one[:, None] == col_one[None, :])
        & (row_two[:, None] == col_two[None, :])
        & (row_live[:, None] > 0)
        & (col_live[None, :] > 0)
    )


def on_device(payload, first_key, second_key, live, first_bucket, second_bucket):
    wide_count = lax.axis_size(WIDE)
    narrow_count = lax.axis_size(NARROW)
    row_count, feature_cols = payload.shape
    slot_rows = row_count // (wide_count * narrow_count)
    owner = first_bucket * narrow_count + second_bucket
    sort_order = jnp.argsort(owner, stable=True)
    inverse = jnp.argsort(sort_order, stable=True)
    sent_rows = payload[sort_order].reshape(wide_count, narrow_count, slot_rows, feature_cols)
    shaped = (wide_count, narrow_count, slot_rows)
    tags = jnp.stack(
        [
            first_key[sort_order].reshape(shaped),
            second_key[sort_order].reshape(shaped),
            live[sort_order].reshape(shaped),
        ],
        axis=2,
    )
    got_rows, got_tags = (
        joined_exchange(sent_rows, WIDE_NARROW, (WIDE, NARROW), (0, 1), (0, 1)),
        joined_exchange(tags, WIDE_NARROW, (WIDE, NARROW), (0, 1), (0, 1)),
    )
    owner_rows = wide_count * narrow_count * slot_rows
    flat_rows = got_rows.reshape(owner_rows, feature_cols)
    keys_one = got_tags[:, :, 0, :].reshape(owner_rows)
    keys_two = got_tags[:, :, 1, :].reshape(owner_rows)
    alive = got_tags[:, :, 2, :].reshape(owner_rows)
    tile_rows = min(512, owner_rows)
    column_pos = lax.iota(jnp.int32, owner_rows)

    def full_block(block_index, running):
        group_means, duplicate_total = running
        block_start = block_index * tile_rows
        row_one = lax.dynamic_slice_in_dim(keys_one, block_start, tile_rows)
        row_two = lax.dynamic_slice_in_dim(keys_two, block_start, tile_rows)
        row_live = lax.dynamic_slice_in_dim(alive, block_start, tile_rows)
        same = pair_mask(row_one, row_two, row_live, keys_one, keys_two, alive)
        sums = jnp.dot(same.astype(jnp.bfloat16), flat_rows, preferred_element_type=jnp.float32)
        counts = jnp.sum(same.astype(jnp.float32), axis=1)
        row_pos = block_start + lax.iota(jnp.int32, tile_rows)
        earlier = same & (column_pos[None, :] < row_pos[:, None])
        duplicate_total = duplicate_total + jnp.sum(jnp.any(earlier, axis=1).astype(jnp.float32))
        block_mean = (sums / jnp.maximum(counts, 1.0)[:, None]).astype(jnp.bfloat16)
        group_means = lax.dynamic_update_slice_in_dim(group_means, block_mean, block_start, 0)
        return (group_means, duplicate_total)

    start_state = (jnp.zeros((owner_rows, feature_cols), jnp.bfloat16), jnp.zeros((), jnp.float32))
    group_means, duplicate_total = lax.fori_loop(
        0, owner_rows // tile_rows, full_block, start_state
    )
    back_rows = group_means.reshape(wide_count, narrow_count, slot_rows, feature_cols)
    returned = joined_exchange(back_rows, WIDE_NARROW, (WIDE, NARROW), (0, 1), (0, 1))
    group_mean = returned.reshape(row_count, feature_cols)[inverse]
    overall = by_axis(duplicate_total, WIDE_NARROW)
    return (group_mean, overall.astype(jnp.int32))


def solution(mesh):
    torus = Mesh(mesh.devices.reshape(8, 4, 4, 2), ("wide_0", "wide_1", "narrow_0", "narrow_1"))
    return jax.shard_map(
        on_device,
        mesh=torus,
        in_specs=(
            P(WIDE_NARROW, None),
            P(WIDE_NARROW),
            P(WIDE_NARROW),
            P(WIDE_NARROW),
            P(WIDE_NARROW),
            P(WIDE_NARROW),
        ),
        out_specs=(P(WIDE_NARROW, None), P()),
        check_vma=False,
    )
```

profile of v0, /device:TPU:1, one launch (start us, length us, event | category | flops | bytes accessed | tf_op | source)
XLA Modules:
  0.0 323.6 jit_solution(10078858872643697720)
XLA Ops:
  1.5 5.8 %sort.31 = (s32[4096]{0:T(1024)}, s32[4096]{0:T(1024)S(1)}) sort(s32[4096]{0:T(1024)S(1)} %multiply_add_fusion, s32[4096]{0:T(1024)S(1)} %iota.19), dimensions={0}, to_apply=%region_0.0 | sort | flops 49152 | bytes 65536 | tf_op jit(solution)/shard_map/jit(argsort)/sort | solution.py:56
  7.3 23.0 %gather_fusion.2 = s32[4096]{0:T(1024)S(1)} fusion(s32[4096]{0:T(1024)S(1)} %copy-done.1, s32[4096]{0:T(1024)S(1)} %fusion.6), kind=kCustom, calls=%fused_computation.2 | custom fusion | bytes 49152 | tf_op jit(solution)/shard_map/gather | solution.py:64
  30.4 23.0 %gather_fusion.1 = s32[4096]{0:T(1024)S(1)} fusion(s32[4096]{0:T(1024)S(1)} %copy-done.2, s32[4096]{0:T(1024)S(1)} %fusion.6), kind=kCustom, calls=%fused_computation.1 | custom fusion | bytes 49152 | tf_op jit(solution)/shard_map/gather | solution.py:63
  53.4 23.0 %gather_fusion = s32[4096]{0:T(1024)S(1)} fusion(s32[4096]{0:T(1024)S(1)} %copy-done.3, s32[4096]{0:T(1024)S(1)} %fusion.6), kind=kCustom, calls=%fused_computation | custom fusion | bytes 49152 | tf_op jit(solution)/shard_map/gather | solution.py:62
  77.9 15.6 %all-to-all-start = ((s32[256,1,1,3,16]{4,2,3,1,0:T(1,128)}), s32[256,1,1,3,16]{4,2,3,1,0:T(1,128)S(1)}, u32[]{:S(2)}, u32[]{:S(2)}) async-start(s32[256,1,1,3,16]{4,2,3,1,0:T(1,128)} %copy.20), calls=%async_computation | async-start | bytes 786432 | tf_op jit(solution)/shard_map/all_to_all | solution.py:30
  93.6 15.0 %gather_fusion.3 = bf16[4096,128]{1,0:T(8,128)(2,1)} fusion(bf16[4096,128]{1,0:T(8,128)(2,1)S(1)} %copy-done, s32[4096]{0:T(1024)S(1)} %fusion.6), kind=kCustom, calls=%fused_computation.3 | custom fusion | bytes 2113536 | tf_op jit(solution)/shard_map/gather | solution.py:58
  110.7 12.7 %all-to-all-start.1 = ((bf16[256,1,1,16,128]{4,3,2,1,0:T(8,128)(2,1)}), bf16[256,1,1,16,128]{4,3,2,1,0:T(8,128)(2,1)}, u32[]{:S(2)}, u32[]{:S(2)}) async-start(bf16[256,1,1,16,128]{4,3,2,1,0:T(8,128)(2,1)} %bitcast.10), calls=%async_computation.1 | async-start | bytes 2097152 | tf_op jit(solution)/shard_map/all_to_all | solution.py:30
  124.0 28.9 %all-to-all-done.1 = bf16[256,1,1,16,128]{4,3,2,1,0:T(8,128)(2,1)} async-done(((bf16[256,1,1,16,128]{4,3,2,1,0:T(8,128)(2,1)}), bf16[256,1,1,16,128]{4,3,2,1,0:T(8,128)(2,1)}, u32[]{:S(2)}, u32[]{:S(2)}) %all-to-all-start.1) | async-done | bytes 1048608 | tf_op jit(solution)/shard_map/all_to_all | solution.py:30
  154.0 79.1 %while.17 = (s32[]{:T(128)}, bf16[4096,128]{1,0:T(8,128)(2,1)}, f32[]{:T(128)}, s32[4096]{0:T(1024)S(1)}, s32[32,8,1,16]{3,1,0,2:T(8,128)}, /*index=5*/s32[4096]...) while((s32[]{:T(128)}, bf16[4096,128]{1,0:T(8,128)(2,1)}, ...), condition=%wide.wide.region_5.6_spmd.clone, body=%wide.wide.region_1.5_spmd.clone.sunk | while | flops 557979136 | bytes 7565543 | solution.py:97
  154.3 4.1 %fusion.21 = (pred[512]{0:T(512)(128)(4,1)S(1)}, pred[512,4096]{1,0:T(32,128)(4,1)S(1)}) fusion(s32[512]{0:T(512)S(1)} %iota_add_fusion.3, pred[4096]{0:T(1024)(128)(4,1)S(1)} %gt.36, pred[512]{0:T(512)(128)(4,1)S(1)} %dynamic-slice_compare_fusion.3, s32[4096]{0:T(1024)S(1)} %get-tuple-element.400, s32[512]{0:T(512)S(1)} %dynamic_slice.32, ...), kind=kLoop, calls=%fused_computation.9.clone.clone.1 | loop fusion | flops 16776704 | bytes 2141184 | tf_op jit(solution)/shard_map/while/body/eval_jaxpr/reduce_or | solution.py:91
  160.7 3.1 fusion.22
  164.2 4.1 %fusion.21 = (pred[512]{0:T(512)(128)(4,1)S(1)}, pred[512,4096]{1,0:T(32,128)(4,1)S(1)}) fusion(s32[512]{0:T(512)S(1)} %iota_add_fusion.3, pred[4096]{0:T(1024)(128)(4,1)S(1)} %gt.36, pred[512]{0:T(512)(128)(4,1)S(1)} %dynamic-slice_compare_fusion.3, s32[4096]{0:T(1024)S(1)} %get-tuple-element.400, s32[512]{0:T(512)S(1)} %dynamic_slice.32, ...), kind=kLoop, calls=%fused_computation.9.clone.clone.1 | loop fusion | flops 16776704 | bytes 2141184 | tf_op jit(solution)/shard_map/while/body/eval_jaxpr/reduce_or | solution.py:91
  170.6 3.1 fusion.22
  174.1 4.1 %fusion.21 = (pred[512]{0:T(512)(128)(4,1)S(1)}, pred[512,4096]{1,0:T(32,128)(4,1)S(1)}) fusion(s32[512]{0:T(512)S(1)} %iota_add_fusion.3, pred[4096]{0:T(1024)(128)(4,1)S(1)} %gt.36, pred[512]{0:T(512)(128)(4,1)S(1)} %dynamic-slice_compare_fusion.3, s32[4096]{0:T(1024)S(1)} %get-tuple-element.400, s32[512]{0:T(512)S(1)} %dynamic_slice.32, ...), kind=kLoop, calls=%fused_computation.9.clone.clone.1 | loop fusion | flops 16776704 | bytes 2141184 | tf_op jit(solution)/shard_map/while/body/eval_jaxpr/reduce_or | solution.py:91
  180.5 3.1 fusion.22
  184.0 4.1 %fusion.21 = (pred[512]{0:T(512)(128)(4,1)S(1)}, pred[512,4096]{1,0:T(32,128)(4,1)S(1)}) fusion(s32[512]{0:T(512)S(1)} %iota_add_fusion.3, pred[4096]{0:T(1024)(128)(4,1)S(1)} %gt.36, pred[512]{0:T(512)(128)(4,1)S(1)} %dynamic-slice_compare_fusion.3, s32[4096]{0:T(1024)S(1)} %get-tuple-element.400, s32[512]{0:T(512)S(1)} %dynamic_slice.32, ...), kind=kLoop, calls=%fused_computation.9.clone.clone.1 | loop fusion | flops 16776704 | bytes 2141184 | tf_op jit(solution)/shard_map/while/body/eval_jaxpr/reduce_or | solution.py:91
  190.3 3.1 fusion.22
  193.9 4.1 %fusion.21 = (pred[512]{0:T(512)(128)(4,1)S(1)}, pred[512,4096]{1,0:T(32,128)(4,1)S(1)}) fusion(s32[512]{0:T(512)S(1)} %iota_add_fusion.3, pred[4096]{0:T(1024)(128)(4,1)S(1)} %gt.36, pred[512]{0:T(512)(128)(4,1)S(1)} %dynamic-slice_compare_fusion.3, s32[4096]{0:T(1024)S(1)} %get-tuple-element.400, s32[512]{0:T(512)S(1)} %dynamic_slice.32, ...), kind=kLoop, calls=%fused_computation.9.clone.clone.1 | loop fusion | flops 16776704 | bytes 2141184 | tf_op jit(solution)/shard_map/while/body/eval_jaxpr/reduce_or | solution.py:91
  200.2 3.1 fusion.22
  203.8 4.1 %fusion.21 = (pred[512]{0:T(512)(128)(4,1)S(1)}, pred[512,4096]{1,0:T(32,128)(4,1)S(1)}) fusion(s32[512]{0:T(512)S(1)} %iota_add_fusion.3, pred[4096]{0:T(1024)(128)(4,1)S(1)} %gt.36, pred[512]{0:T(512)(128)(4,1)S(1)} %dynamic-slice_compare_fusion.3, s32[4096]{0:T(1024)S(1)} %get-tuple-element.400, s32[512]{0:T(512)S(1)} %dynamic_slice.32, ...), kind=kLoop, calls=%fused_computation.9.clone.clone.1 | loop fusion | flops 16776704 | bytes 2141184 | tf_op jit(solution)/shard_map/while/body/eval_jaxpr/reduce_or | solution.py:91
  210.1 3.1 fusion.22
  213.6 4.1 %fusion.21 = (pred[512]{0:T(512)(128)(4,1)S(1)}, pred[512,4096]{1,0:T(32,128)(4,1)S(1)}) fusion(s32[512]{0:T(512)S(1)} %iota_add_fusion.3, pred[4096]{0:T(1024)(128)(4,1)S(1)} %gt.36, pred[512]{0:T(512)(128)(4,1)S(1)} %dynamic-slice_compare_fusion.3, s32[4096]{0:T(1024)S(1)} %get-tuple-element.400, s32[512]{0:T(512)S(1)} %dynamic_slice.32, ...), kind=kLoop, calls=%fused_computation.9.clone.clone.1 | loop fusion | flops 16776704 | bytes 2141184 | tf_op jit(solution)/shard_map/while/body/eval_jaxpr/reduce_or | solution.py:91
  220.0 3.1 fusion.22
  223.5 4.1 %fusion.21 = (pred[512]{0:T(512)(128)(4,1)S(1)}, pred[512,4096]{1,0:T(32,128)(4,1)S(1)}) fusion(s32[512]{0:T(512)S(1)} %iota_add_fusion.3, pred[4096]{0:T(1024)(128)(4,1)S(1)} %gt.36, pred[512]{0:T(512)(128)(4,1)S(1)} %dynamic-slice_compare_fusion.3, s32[4096]{0:T(1024)S(1)} %get-tuple-element.400, s32[512]{0:T(512)S(1)} %dynamic_slice.32, ...), kind=kLoop, calls=%fused_computation.9.clone.clone.1 | loop fusion | flops 16776704 | bytes 2141184 | tf_op jit(solution)/shard_map/while/body/eval_jaxpr/reduce_or | solution.py:91
  229.9 3.1 fusion.22
  233.0 6.7 %all-to-all-start.2 = ((bf16[256,1,1,16,128]{4,3,2,1,0:T(8,128)(2,1)}), bf16[256,1,1,16,128]{4,3,2,1,0:T(8,128)(2,1)S(1)}, u32[]{:S(2)}, u32[]{:S(2)}) async-start(bf16[256,1,1,16,128]{4,3,2,1,0:T(8,128)(2,1)} %bitcast.66), calls=%async_computation.2 | async-start | bytes 2097152 | tf_op jit(solution)/shard_map/all_to_all | solution.py:30
  239.8 33.2 %psum.28 = f32[]{:T(128)} all-reduce(f32[]{:T(128)} %get-tuple-element.192), channel_id=1, replica_groups=mesh['wide_0'=8,'wide_1'=4,'narrow_0'=4,'narrow_1'=2] {'wide_0'}, use_global_device_ids=true, to_apply=%region_7.8 | all-reduce | flops 1 | bytes 8 | tf_op jit(solution)/shard_map/psum | solution.py:37
  272.9 8.6 %psum.29 = f32[]{:T(128)} all-reduce(f32[]{:T(128)} %psum.28), channel_id=1, replica_groups=mesh['wide_0'=8,'wide_1'=4,'narrow_0'=4,'narrow_1'=2] {'wide_1'}, use_global_device_ids=true, to_apply=%region_8.9 | all-reduce | flops 1 | bytes 8 | tf_op jit(solution)/shard_map/psum | solution.py:37
  281.5 5.8 %sort.32 = (s32[4096]{0:T(1024)}, s32[4096]{0:T(1024)S(1)}) sort(s32[4096]{0:T(1024)S(1)} %get-tuple-element.189, s32[4096]{0:T(1024)S(1)} %iota.21), dimensions={0}, to_apply=%region_6.7 | sort | flops 49152 | bytes 65536 | tf_op jit(solution)/shard_map/jit(argsort)/sort | solution.py:57
  287.3 9.1 %psum.30 = f32[]{:T(128)} all-reduce(f32[]{:T(128)} %psum.29), channel_id=1, replica_groups=mesh['wide_0'=8,'wide_1'=4,'narrow_0'=4,'narrow_1'=2] {'narrow_0'}, use_global_device_ids=true, to_apply=%region_9.10 | all-reduce | flops 1 | bytes 8 | tf_op jit(solution)/shard_map/psum | solution.py:37
  296.5 10.3 %psum.31 = f32[]{:T(128)} all-reduce(f32[]{:T(128)} %psum.30), channel_id=1, replica_groups=mesh['wide_0'=8,'wide_1'=4,'narrow_0'=4,'narrow_1'=2] {'narrow_1'}, use_global_device_ids=true, to_apply=%region_10.11 | all-reduce | flops 1 | bytes 8 | tf_op jit(solution)/shard_map/psum | solution.py:37
  307.5 15.0 %gather_fusion.4 = bf16[4096,128]{1,0:T(8,128)(2,1)} fusion(bf16[4096,128]{1,0:T(8,128)(2,1)S(1)} %bitcast.65, s32[4096]{0:T(1024)S(1)} %fusion.7), kind=kCustom, calls=%fused_computation.4 | custom fusion | bytes 2113536 | tf_op jit(solution)/shard_map/gather | solution.py:102
  (104 shorter events, 21.6 us)
Async XLA Ops:
  0.6 93.0 %copy-start = (bf16[4096,128]{1,0:T(8,128)(2,1)S(1)}, bf16[4096,128]{1,0:T(8,128)(2,1)}, u32[]{:S(2)}) copy-start(bf16[4096,128]{1,0:T(8,128)(2,1)} %param.8) | copy-start | bytes 3145732
  0.6 6.6 %copy-start.1 = (s32[4096]{0:T(1024)S(1)}, s32[4096]{0:T(1024)}, u32[]{:S(2)}) copy-start(s32[4096]{0:T(1024)} %param.11) | copy-start | bytes 49156
  7.3 23.1 %copy-start.2 = (s32[4096]{0:T(1024)S(1)}, s32[4096]{0:T(1024)}, u32[]{:S(2)}) copy-start(s32[4096]{0:T(1024)} %param.10) | copy-start | bytes 49156
  30.3 23.1 %copy-start.3 = (s32[4096]{0:T(1024)S(1)}, s32[4096]{0:T(1024)}, u32[]{:S(2)}) copy-start(s32[4096]{0:T(1024)} %param.9) | copy-start | bytes 49156
  77.9 32.7 %all-to-all-start = ((s32[256,1,1,3,16]{4,2,3,1,0:T(1,128)}), s32[256,1,1,3,16]{4,2,3,1,0:T(1,128)S(1)}, u32[]{:S(2)}, u32[]{:S(2)}) async-start(s32[256,1,1,3,16]{4,2,3,1,0:T(1,128)} %copy.20), calls=%async_computation | async-start | bytes 786432 | tf_op jit(solution)/shard_map/all_to_all | solution.py:30
  110.7 42.2 %all-to-all-start.1 = ((bf16[256,1,1,16,128]{4,3,2,1,0:T(8,128)(2,1)}), bf16[256,1,1,16,128]{4,3,2,1,0:T(8,128)(2,1)}, u32[]{:S(2)}, u32[]{:S(2)}) async-start(bf16[256,1,1,16,128]{4,3,2,1,0:T(8,128)(2,1)} %bitcast.10), calls=%async_computation.1 | async-start | bytes 2097152 | tf_op jit(solution)/shard_map/all_to_all | solution.py:30
  123.4 30.5 %copy-start.4 = (s32[32,8,1,16]{3,1,0,2:T(8,128)}, s32[32,8,1,16]{3,1,0,2:T(8,128)S(1)}, u32[]{:S(2)}) copy-start(s32[32,8,1,16]{3,1,0,2:T(8,128)S(1)} %get-tuple-element.364) | copy-start | bytes 49156
  123.4 30.5 %copy-start.5 = (s32[32,8,1,16]{3,1,0,2:T(8,128)}, s32[32,8,1,16]{3,1,0,2:T(8,128)S(1)}, u32[]{:S(2)}) copy-start(s32[32,8,1,16]{3,1,0,2:T(8,128)S(1)} %get-tuple-element.362) | copy-start | bytes 49156
  233.0 74.4 %all-to-all-start.2 = ((bf16[256,1,1,16,128]{4,3,2,1,0:T(8,128)(2,1)}), bf16[256,1,1,16,128]{4,3,2,1,0:T(8,128)(2,1)S(1)}, u32[]{:S(2)}, u32[]{:S(2)}) async-start(bf16[256,1,1,16,128]{4,3,2,1,0:T(8,128)(2,1)} %bitcast.66), calls=%async_computation.2 | async-start | bytes 2097152 | tf_op jit(solution)/shard_map/all_to_all | solution.py:30
where the time goes:
time: 324 us
  local copies, waits for them, and re-layouts  104 us (32%)
  blocking collectives  61.2 us (19%)
  other arithmetic  59 us (18%)
  starting transfers between devices  35 us (11%)
  waiting for transfers between devices  30.9 us (10%)
  matrix products  25.2 us (8%)
  loops' own time  5.22 us (2%)
    psum x4, blocking collectives, by_axis(): array = lax.psum(array, axis)  61.2 us
    all_to_all x3, starting transfers between devices, joined_exchange(): lax.all_to_all(pieces, axis, split_axis=0, concat_axis=0, tiled=True)  35 us
    reduce_or x8, other arithmetic, full_block(): jnp.any(earlier, axis=1).astype(jnp.float32)  33.1 us
    all_to_all x3, waiting for transfers between devices, joined_exchange(): lax.all_to_all(pieces, axis, split_axis=0, concat_axis=0, tiled=True)  30.9 us
    dot_general x8, matrix products, full_block(): jnp.dot(same.astype(jnp.bfloat16), flat_rows, preferred_element_type=jnp....  25.2 us
    gather x1, local copies, waits for them, and re-layouts, on_device(): live[sort_order].reshape(shaped)  23 us
    gather x1, local copies, waits for them, and re-layouts, on_device(): second_key[sort_order].reshape(shaped)  23 us
    gather x1, local copies, waits for them, and re-layouts, on_device(): first_key[sort_order].reshape(shaped)  23 us
  transfers between devices with their start and end apart: 3, of which 2 were waited for; matrix products, arithmetic and copies ran while one was open for 7% of the time, Pallas kernels for 0%

commit v1 on v0

--- a/solution.py
+++ b/solution.py
@@ -7,6 +7,12 @@
 WIDE = ("wide_0", "wide_1")
 NARROW = ("narrow_0", "narrow_1")
 WIDE_NARROW = ("wide_0", "wide_1", "narrow_0", "narrow_1")
+
+
+def gather_and_add(x, mesh_axis):
+    blocks = lax.all_gather(x, mesh_axis, axis=0, tiled=False)
+    summed = blocks.sum(axis=0)
+    return summed
 
 
 def in_blocks(array, dim, length):
@@ -34,7 +40,7 @@
 
 def by_axis(array, axes):
     for axis in axes:
-        array = lax.psum(array, axis)
+        array = gather_and_add(array, axis)
     return array
 
 

time: 324 us -> 316 us (0.975)
  blocking collectives: 61.2 us -> 50.9 us
  matrix products: 25.2 us -> 15.4 us
  local copies, waits for them, and re-layouts: 104 us -> 113 us
    psum x4 -> x0, blocking collectives: 61.2 us -> none  [by_axis(): array = lax.psum(array, axis)]
    unnamed x0 -> x4, blocking collectives: none -> 50.9 us
    dot_general x8, matrix products: 25.2 us -> 15.4 us  [full_block(): jnp.dot(same.astype(jnp.bfloat16), flat_rows, preferred_element_type=jnp....]
    unnamed x12 -> x32, local copies, waits for them, and re-layouts: 0.03 us -> 8.94 us
  transfers between devices with their start and end apart: 3 -> 3, of which waited for: 2 -> 2; matrix products, arithmetic and copies ran while one was open for 7% -> 10% of each run, Pallas kernels for 0% -> 0%
where the time goes in v1:
time: 316 us
  local copies, waits for them, and re-layouts  113 us (36%)
  other arithmetic  61.9 us (20%)
  blocking collectives  50.9 us (16%)
  starting transfers between devices  34 us (11%)
  waiting for transfers between devices  31.8 us (10%)
  matrix products  15.4 us (5%)
  loops' own time  5.46 us (2%)
    unnamed x4, blocking collectives  50.9 us
    all_to_all x3, starting transfers between devices, joined_exchange(): lax.all_to_all(pieces, axis, split_axis=0, concat_axis=0, tiled=True)  34 us
    reduce_or x8, other arithmetic, full_block(): jnp.any(earlier, axis=1).astype(jnp.float32)  33.1 us
    all_to_all x3, waiting for transfers between devices, joined_exchange(): lax.all_to_all(pieces, axis, split_axis=0, concat_axis=0, tiled=True)  31.8 us
    gather x1, local copies, waits for them, and re-layouts, on_device(): second_key[sort_order].reshape(shaped)  23 us
    gather x1, local copies, waits for them, and re-layouts, on_device(): live[sort_order].reshape(shaped)  23 us
    gather x1, local copies, waits for them, and re-layouts, on_device(): first_key[sort_order].reshape(shaped)  23 us
    dot_general x8, matrix products, full_block(): jnp.dot(same.astype(jnp.bfloat16), flat_rows, preferred_element_type=jnp....  15.4 us
  transfers between devices with their start and end apart: 3, of which 2 were waited for; matrix products, arithmetic and copies ran while one was open for 10% of the time, Pallas kernels for 0%

profile of v1, /device:TPU:1, one launch (start us, length us, event | category | flops | bytes accessed | tf_op | source)
XLA Modules:
  0.0 315.5 jit_solution(14667869075532979340)
XLA Ops:
  1.5 5.8 %sort.31 = (s32[4096]{0:T(1024)}, s32[4096]{0:T(1024)S(1)}) sort(s32[4096]{0:T(1024)S(1)} %multiply_add_fusion, s32[4096]{0:T(1024)S(1)} %iota.19), dimensions={0}, to_apply=%region_0.0 | sort | flops 49152 | bytes 65536 | tf_op jit(solution)/shard_map/jit(argsort)/sort | solution.py:62
  7.3 23.0 %gather_fusion.1 = s32[4096]{0:T(1024)S(1)} fusion(s32[4096]{0:T(1024)S(1)} %copy-done.1, s32[4096]{0:T(1024)S(1)} %fusion.6), kind=kCustom, calls=%fused_computation.1 | custom fusion | bytes 49152 | tf_op jit(solution)/shard_map/gather | solution.py:69
  31.0 23.0 %gather_fusion.2 = s32[4096]{0:T(1024)S(1)} fusion(s32[4096]{0:T(1024)S(1)} %copy-done.2, s32[4096]{0:T(1024)S(1)} %fusion.6), kind=kCustom, calls=%fused_computation.2 | custom fusion | bytes 49152 | tf_op jit(solution)/shard_map/gather | solution.py:70
  54.8 23.0 %gather_fusion = s32[4096]{0:T(1024)S(1)} fusion(s32[4096]{0:T(1024)S(1)} %copy-done.3, s32[4096]{0:T(1024)S(1)} %fusion.6), kind=kCustom, calls=%fused_computation | custom fusion | bytes 49152 | tf_op jit(solution)/shard_map/gather | solution.py:68
  79.1 15.6 %all-to-all-start = ((s32[256,1,1,3,16]{4,2,3,1,0:T(1,128)}), s32[256,1,1,3,16]{4,2,3,1,0:T(1,128)S(1)}, u32[]{:S(2)}, u32[]{:S(2)}) async-start(s32[256,1,1,3,16]{4,2,3,1,0:T(1,128)} %copy.20), calls=%async_computation | async-start | bytes 786432 | tf_op jit(solution)/shard_map/all_to_all | solution.py:36
  94.8 15.0 %gather_fusion.3 = bf16[4096,128]{1,0:T(8,128)(2,1)} fusion(bf16[4096,128]{1,0:T(8,128)(2,1)S(1)} %copy-done, s32[4096]{0:T(1024)S(1)} %fusion.6), kind=kCustom, calls=%fused_computation.3 | custom fusion | bytes 2113536 | tf_op jit(solution)/shard_map/gather | solution.py:64
  109.8 2.0 all-to-all-done
  111.9 11.7 %all-to-all-start.1 = ((bf16[256,1,1,16,128]{4,3,2,1,0:T(8,128)(2,1)}), bf16[256,1,1,16,128]{4,3,2,1,0:T(8,128)(2,1)S(1)}, u32[]{:S(2)}, u32[]{:S(2)}) async-start(bf16[256,1,1,16,128]{4,3,2,1,0:T(8,128)(2,1)} %bitcast.10), calls=%async_computation.1 | async-start | bytes 2097152 | tf_op jit(solution)/shard_map/all_to_all | solution.py:36
  124.1 29.8 %all-to-all-done.1 = bf16[256,1,1,16,128]{4,3,2,1,0:T(8,128)(2,1)S(1)} async-done(((bf16[256,1,1,16,128]{4,3,2,1,0:T(8,128)(2,1)}), bf16[256,1,1,16,128]{4,3,2,1,0:T(8,128)(2,1)S(1)}, u32[]{:S(2)}, u32[]{:S(2)}) %all-to-all-start.1) | async-done | bytes 1048608 | tf_op jit(solution)/shard_map/all_to_all | solution.py:36
  155.0 69.9 %while.17 = (s32[]{:T(128)}, bf16[4096,128]{1,0:T(8,128)(2,1)}, f32[]{:T(128)}, s32[4096]{0:T(1024)S(1)}, s32[32,8,1,16]{3,1,0,2:T(8,128)}, /*index=5*/s32[4096]...) while((s32[]{:T(128)}, bf16[4096,128]{1,0:T(8,128)(2,1)}, ...), condition=%wide.wide.region_5.6_spmd.clone, body=%wide.wide.region_1.5_spmd.clone.sunk | while | flops 557979136 | bytes 7565543 | solution.py:103
  155.4 4.1 %fusion.21 = (pred[512]{0:T(512)(128)(4,1)S(1)}, pred[512,4096]{1,0:T(32,128)(4,1)S(1)}) fusion(s32[512]{0:T(512)S(1)} %iota_add_fusion.3, pred[4096]{0:T(1024)(128)(4,1)S(1)} %gt.36, pred[512]{0:T(512)(128)(4,1)S(1)} %dynamic-slice_compare_fusion.3, s32[4096]{0:T(1024)S(1)} %get-tuple-element.400, s32[512]{0:T(512)S(1)} %dynamic_slice.32, ...), kind=kLoop, calls=%fused_computation.9.clone.clone.1 | loop fusion | flops 16776704 | bytes 2141184 | tf_op jit(solution)/shard_map/while/body/eval_jaxpr/reduce_or | solution.py:97
  160.6 1.9 fusion.22
  164.2 4.1 %fusion.21 = (pred[512]{0:T(512)(128)(4,1)S(1)}, pred[512,4096]{1,0:T(32,128)(4,1)S(1)}) fusion(s32[512]{0:T(512)S(1)} %iota_add_fusion.3, pred[4096]{0:T(1024)(128)(4,1)S(1)} %gt.36, pred[512]{0:T(512)(128)(4,1)S(1)} %dynamic-slice_compare_fusion.3, s32[4096]{0:T(1024)S(1)} %get-tuple-element.400, s32[512]{0:T(512)S(1)} %dynamic_slice.32, ...), kind=kLoop, calls=%fused_computation.9.clone.clone.1 | loop fusion | flops 16776704 | bytes 2141184 | tf_op jit(solution)/shard_map/while/body/eval_jaxpr/reduce_or | solution.py:97
  169.3 1.9 fusion.22
  172.9 4.1 %fusion.21 = (pred[512]{0:T(512)(128)(4,1)S(1)}, pred[512,4096]{1,0:T(32,128)(4,1)S(1)}) fusion(s32[512]{0:T(512)S(1)} %iota_add_fusion.3, pred[4096]{0:T(1024)(128)(4,1)S(1)} %gt.36, pred[512]{0:T(512)(128)(4,1)S(1)} %dynamic-slice_compare_fusion.3, s32[4096]{0:T(1024)S(1)} %get-tuple-element.400, s32[512]{0:T(512)S(1)} %dynamic_slice.32, ...), kind=kLoop, calls=%fused_computation.9.clone.clone.1 | loop fusion | flops 16776704 | bytes 2141184 | tf_op jit(solution)/shard_map/while/body/eval_jaxpr/reduce_or | solution.py:97
  178.1 1.9 fusion.22
  181.6 4.1 %fusion.21 = (pred[512]{0:T(512)(128)(4,1)S(1)}, pred[512,4096]{1,0:T(32,128)(4,1)S(1)}) fusion(s32[512]{0:T(512)S(1)} %iota_add_fusion.3, pred[4096]{0:T(1024)(128)(4,1)S(1)} %gt.36, pred[512]{0:T(512)(128)(4,1)S(1)} %dynamic-slice_compare_fusion.3, s32[4096]{0:T(1024)S(1)} %get-tuple-element.400, s32[512]{0:T(512)S(1)} %dynamic_slice.32, ...), kind=kLoop, calls=%fused_computation.9.clone.clone.1 | loop fusion | flops 16776704 | bytes 2141184 | tf_op jit(solution)/shard_map/while/body/eval_jaxpr/reduce_or | solution.py:97
  186.8 1.9 fusion.22
  190.4 4.1 %fusion.21 = (pred[512]{0:T(512)(128)(4,1)S(1)}, pred[512,4096]{1,0:T(32,128)(4,1)S(1)}) fusion(s32[512]{0:T(512)S(1)} %iota_add_fusion.3, pred[4096]{0:T(1024)(128)(4,1)S(1)} %gt.36, pred[512]{0:T(512)(128)(4,1)S(1)} %dynamic-slice_compare_fusion.3, s32[4096]{0:T(1024)S(1)} %get-tuple-element.400, s32[512]{0:T(512)S(1)} %dynamic_slice.32, ...), kind=kLoop, calls=%fused_computation.9.clone.clone.1 | loop fusion | flops 16776704 | bytes 2141184 | tf_op jit(solution)/shard_map/while/body/eval_jaxpr/reduce_or | solution.py:97
  195.5 1.9 fusion.22
  199.1 4.1 %fusion.21 = (pred[512]{0:T(512)(128)(4,1)S(1)}, pred[512,4096]{1,0:T(32,128)(4,1)S(1)}) fusion(s32[512]{0:T(512)S(1)} %iota_add_fusion.3, pred[4096]{0:T(1024)(128)(4,1)S(1)} %gt.36, pred[512]{0:T(512)(128)(4,1)S(1)} %dynamic-slice_compare_fusion.3, s32[4096]{0:T(1024)S(1)} %get-tuple-element.400, s32[512]{0:T(512)S(1)} %dynamic_slice.32, ...), kind=kLoop, calls=%fused_computation.9.clone.clone.1 | loop fusion | flops 16776704 | bytes 2141184 | tf_op jit(solution)/shard_map/while/body/eval_jaxpr/reduce_or | solution.py:97
  204.3 1.9 fusion.22
  207.9 4.1 %fusion.21 = (pred[512]{0:T(512)(128)(4,1)S(1)}, pred[512,4096]{1,0:T(32,128)(4,1)S(1)}) fusion(s32[512]{0:T(512)S(1)} %iota_add_fusion.3, pred[4096]{0:T(1024)(128)(4,1)S(1)} %gt.36, pred[512]{0:T(512)(128)(4,1)S(1)} %dynamic-slice_compare_fusion.3, s32[4096]{0:T(1024)S(1)} %get-tuple-element.400, s32[512]{0:T(512)S(1)} %dynamic_slice.32, ...), kind=kLoop, calls=%fused_computation.9.clone.clone.1 | loop fusion | flops 16776704 | bytes 2141184 | tf_op jit(solution)/shard_map/while/body/eval_jaxpr/reduce_or | solution.py:97
  216.6 4.1 %fusion.21 = (pred[512]{0:T(512)(128)(4,1)S(1)}, pred[512,4096]{1,0:T(32,128)(4,1)S(1)}) fusion(s32[512]{0:T(512)S(1)} %iota_add_fusion.3, pred[4096]{0:T(1024)(128)(4,1)S(1)} %gt.36, pred[512]{0:T(512)(128)(4,1)S(1)} %dynamic-slice_compare_fusion.3, s32[4096]{0:T(1024)S(1)} %get-tuple-element.400, s32[512]{0:T(512)S(1)} %dynamic_slice.32, ...), kind=kLoop, calls=%fused_computation.9.clone.clone.1 | loop fusion | flops 16776704 | bytes 2141184 | tf_op jit(solution)/shard_map/while/body/eval_jaxpr/reduce_or | solution.py:97
  221.8 1.9 fusion.22
  225.0 6.7 %all-to-all-start.2 = ((bf16[256,1,1,16,128]{4,3,2,1,0:T(8,128)(2,1)}), bf16[256,1,1,16,128]{4,3,2,1,0:T(8,128)(2,1)S(1)}, u32[]{:S(2)}, u32[]{:S(2)}) async-start(bf16[256,1,1,16,128]{4,3,2,1,0:T(8,128)(2,1)} %bitcast.16), calls=%async_computation.2 | async-start | bytes 2097152 | tf_op jit(solution)/shard_map/all_to_all | solution.py:36
  231.8 5.8 %sort.32 = (s32[4096]{0:T(1024)}, s32[4096]{0:T(1024)S(1)}) sort(s32[4096]{0:T(1024)S(1)} %get-tuple-element.189, s32[4096]{0:T(1024)S(1)} %iota.21), dimensions={0}, to_apply=%region_6.7 | sort | flops 49152 | bytes 65536 | tf_op jit(solution)/shard_map/jit(argsort)/sort | solution.py:63
  239.6 24.9 %all-reduce = f32[8]{0:T(128)S(1)} all-reduce(f32[8]{0:T(128)S(1)} %dynamic-update-slice), channel_id=1, replica_groups=mesh['wide_0'=8,'wide_1'=4,'narrow_0'=4,'narrow_1'=2] {'wide_0'}, use_global_device_ids=true, to_apply=%add | all-reduce | flops 8 | bytes 64
  267.1 8.0 %all-reduce.1 = f32[4]{0:T(128)S(1)} all-reduce(f32[4]{0:T(128)S(1)} %dynamic-update-slice.1), channel_id=1, replica_groups=mesh['wide_0'=8,'wide_1'=4,'narrow_0'=4,'narrow_1'=2] {'wide_1'}, use_global_device_ids=true, to_apply=%add.1 | all-reduce | flops 4 | bytes 32
  277.8 8.5 %all-reduce.2 = f32[4]{0:T(128)S(1)} all-reduce(f32[4]{0:T(128)S(1)} %dynamic-update-slice.2), channel_id=1, replica_groups=mesh['wide_0'=8,'wide_1'=4,'narrow_0'=4,'narrow_1'=2] {'narrow_0'}, use_global_device_ids=true, to_apply=%add.2 | all-reduce | flops 4 | bytes 32
  288.4 9.6 %all-reduce.3 = f32[2]{0:T(128)S(1)} all-reduce(f32[2]{0:T(128)S(1)} %dynamic-update-slice.3), channel_id=1, replica_groups=mesh['wide_0'=8,'wide_1'=4,'narrow_0'=4,'narrow_1'=2] {'narrow_1'}, use_global_device_ids=true, to_apply=%add.3 | all-reduce | flops 2 | bytes 16
  299.4 15.0 %gather_fusion.4 = bf16[4096,128]{1,0:T(8,128)(2,1)} fusion(bf16[4096,128]{1,0:T(8,128)(2,1)S(1)} %bitcast.73, s32[4096]{0:T(1024)S(1)} %fusion.7), kind=kCustom, calls=%fused_computation.4 | custom fusion | bytes 2113536 | tf_op jit(solution)/shard_map/gather | solution.py:108
  (128 shorter events, 33.3 us)
Async XLA Ops:
  0.6 94.1 %copy-start = (bf16[4096,128]{1,0:T(8,128)(2,1)S(1)}, bf16[4096,128]{1,0:T(8,128)(2,1)}, u32[]{:S(2)}) copy-start(bf16[4096,128]{1,0:T(8,128)(2,1)} %param.8) | copy-start | bytes 3145732
  0.6 6.6 %copy-start.1 = (s32[4096]{0:T(1024)S(1)}, s32[4096]{0:T(1024)}, u32[]{:S(2)}) copy-start(s32[4096]{0:T(1024)} %param.10) | copy-start | bytes 49156
  30.3 0.7 copy-start.2
  54.1 0.7 copy-start.3
  79.1 32.7 %all-to-all-start = ((s32[256,1,1,3,16]{4,2,3,1,0:T(1,128)}), s32[256,1,1,3,16]{4,2,3,1,0:T(1,128)S(1)}, u32[]{:S(2)}, u32[]{:S(2)}) async-start(s32[256,1,1,3,16]{4,2,3,1,0:T(1,128)} %copy.20), calls=%async_computation | async-start | bytes 786432 | tf_op jit(solution)/shard_map/all_to_all | solution.py:36
  111.9 42.1 %all-to-all-start.1 = ((bf16[256,1,1,16,128]{4,3,2,1,0:T(8,128)(2,1)}), bf16[256,1,1,16,128]{4,3,2,1,0:T(8,128)(2,1)S(1)}, u32[]{:S(2)}, u32[]{:S(2)}) async-start(bf16[256,1,1,16,128]{4,3,2,1,0:T(8,128)(2,1)} %bitcast.10), calls=%async_computation.1 | async-start | bytes 2097152 | tf_op jit(solution)/shard_map/all_to_all | solution.py:36
  123.6 31.4 %copy-start.4 = (s32[32,8,1,16]{3,1,0,2:T(8,128)}, s32[32,8,1,16]{3,1,0,2:T(8,128)S(1)}, u32[]{:S(2)}) copy-start(s32[32,8,1,16]{3,1,0,2:T(8,128)S(1)} %get-tuple-element.364) | copy-start | bytes 49156
  123.6 31.4 %copy-start.5 = (s32[32,8,1,16]{3,1,0,2:T(8,128)}, s32[32,8,1,16]{3,1,0,2:T(8,128)S(1)}, u32[]{:S(2)}) copy-start(s32[32,8,1,16]{3,1,0,2:T(8,128)S(1)} %get-tuple-element.362) | copy-start | bytes 49156
  225.0 12.6 %copy-start.9 = (u32[256]{0:T(256)S(1)}, u32[256]{0:T(256)}, u32[]{:S(2)}) copy-start(u32[256]{0:T(256)} %constant.61) | copy-start | bytes 3076
  225.0 13.9 %copy-start.8 = (u32[256]{0:T(256)S(1)}, u32[256]{0:T(256)}, u32[]{:S(2)}) copy-start(u32[256]{0:T(256)} %constant.66) | copy-start | bytes 3076
  225.0 41.5 %copy-start.7 = (u32[256]{0:T(256)S(1)}, u32[256]{0:T(256)}, u32[]{:S(2)}) copy-start(u32[256]{0:T(256)} %constant.71) | copy-start | bytes 3076
  225.0 52.2 %copy-start.6 = (u32[256]{0:T(256)S(1)}, u32[256]{0:T(256)}, u32[]{:S(2)}) copy-start(u32[256]{0:T(256)} %constant.76) | copy-start | bytes 3076
  225.0 74.4 %all-to-all-start.2 = ((bf16[256,1,1,16,128]{4,3,2,1,0:T(8,128)(2,1)}), bf16[256,1,1,16,128]{4,3,2,1,0:T(8,128)(2,1)S(1)}, u32[]{:S(2)}, u32[]{:S(2)}) async-start(bf16[256,1,1,16,128]{4,3,2,1,0:T(8,128)(2,1)} %bitcast.16), calls=%async_computation.2 | async-start | bytes 2097152 | tf_op jit(solution)/shard_map/all_to_all | solution.py:36
